TPU v7x, 32 devices: a whole 2x2x4 slice. The times are simulated.
32 devices in a mesh: groups: 2 (over y), seq: 4 (over z), exp: 2 (over x), tp: 2 (over core).
Axes of the slice: x: 2, y: 2, z: 4, core: 2. Of those that a mesh axis runs over, the one named last changes fastest.
Arguments:
- attn_query: bfloat16 [2048, 1152], P(('groups', 'seq'), ('exp', 'tp')), parts along dimension 0, may hold values from -6 to 6
- fresh_keys: bfloat16 [2048, 1152], P(('groups', 'seq'), ('exp', 'tp')), parts along dimension 0, may hold values from -6 to 6
- fresh_values: bfloat16 [2048, 1152], P(('groups', 'seq'), ('exp', 'tp')), parts along dimension 0, may hold values from -6 to 6
- stale_keys: bfloat16 [2048, 1152], P(('groups', 'seq'), ('exp', 'tp')), parts along dimension 0, may hold values from -6 to 6
- stale_values: bfloat16 [2048, 1152], P(('groups', 'seq'), ('exp', 'tp')), parts along dimension 0, may hold values from -6 to 6
- block_flags: int32 [16], P(('groups', 'seq')), parts along dimension 0, may hold values 0 or 1
- moe_tokens: bfloat16 [4096, 1152], P(('groups', 'seq', 'exp', 'tp')), parts along dimension 0, may hold values from -6 to 6
- expert_ids: int32 [4096, 2], P(('groups', 'seq', 'exp', 'tp')), parts along dimension 0, may hold values from 0 to 3, all different within a row; in each aligned block of 128 rows (0 to 127, 128 to 255, ...) at most 80 rows name the same one
- gate_weights: float32 [4096, 2], P(('groups', 'seq', 'exp', 'tp')), parts along dimension 0, may hold values from 0.25 to 1
- up_weight: bfloat16 [4, 1152, 4608], P('seq', None, ('exp', 'tp')), may hold values from -0.1875 to 0.1875
- up_bias: float32 [4, 4608], P('seq', ('exp', 'tp')), may hold values from -3 to 3
- down_weight: bfloat16 [4, 4608, 1152], P('seq', ('exp', 'tp')), may hold values from -0.09375 to 0.09375
- down_bias: float32 [4, 1152], P('seq'), may hold values from -2 to 2
Outputs:
- attn_out: bfloat16 [2048, 1152], P(('groups', 'seq'), ('exp', 'tp')), parts along dimension 0
- moe_out: bfloat16 [4096, 1152], P(('groups', 'seq', 'exp', 'tp')), parts along dimension 0
There are 2 independent parts, one for each index of `groups`. A program takes and returns all parts, laid end to end along the dimension named above; an argument that names none is the same for every part. Nothing has to cross between parts.
Inputs may be any that keep to these rules, and one draw needn't show every extreme that they name: `expert_ids`: the 2 ids of a token differ. In the rows of one device no expert is named more than 80 times, and in every draw some expert is named exactly 80 times in some device's rows.
All inputs are finite; a program needn't handle non-finite values. No bound on the sum of `block_flags` on one device may be relied on, other than what follows from the above.
Results may differ from a plain program's by a relative error of at most 0.014.
Values may be sent and summed in bfloat16 or wider, within the bound.
A program may use at most 64 MiB of HBM per device.

v0:
```python
import math
import jax
import jax.numpy as jnp
from jax import lax
from jax.sharding import PartitionSpec as P

HD = 72


def over_all_2(share, axis, dim, apply):
    everything = lax.all_gather(share, axis, axis=dim, tiled=True)
    return apply(everything, jnp.int32(0))


def attention_part(attn_query, fresh_keys, fresh_values, stale_keys, stale_values, block_flags):
    length = attn_query.shape[0]
    heads_here = attn_query.shape[1] // HD
    row_flags = (jnp.repeat(block_flags, length // block_flags.shape[0]) == 1)[:, None]
    keys = jnp.where(row_flags, fresh_keys, stale_keys)
    values = jnp.where(row_flags, fresh_values, stale_values)
    queries = attn_query.reshape(length, heads_here, HD)
    scale = 1.0 / math.sqrt(HD)
    initial = (
        jnp.full((heads_here, length), -1e30, jnp.float32),
        jnp.zeros((heads_here, length), jnp.float32),
        jnp.zeros((heads_here, length, HD), jnp.float32),
    )
    carry = initial
    piece = (
        lax.all_gather(keys, "seq", axis=0, tiled=True),
        lax.all_gather(values, "seq", axis=0, tiled=True),
    )
    count = piece[0].shape[0]
    width = math.gcd(count, 512)
    key_blocks = piece[0].reshape(count // width, width, heads_here, HD)
    value_blocks = piece[1].reshape(count // width, width, heads_here, HD)

    def advance(state, blocks):
        highest, totals, weighted = state
        key_block, value_block = blocks
        scores = (
            jnp.einsum("qhd,khd->hqk", queries, key_block, preferred_element_type=jnp.float32)
            * scale
        )
        new_high = jnp.maximum(highest, jnp.max(scores, axis=-1))
        rescale = jnp.exp(highest - new_high)
        probs = jnp.exp(scores - new_high[:, :, None])
        totals = totals * rescale + jnp.sum(probs, axis=-1)
        weighted = weighted * rescale[:, :, None] + jnp.einsum(
            "hqk,khd->hqd",
            probs.astype(jnp.bfloat16),
            value_block,
            preferred_element_type=jnp.float32,
        )
        return ((new_high, totals, weighted), None)

    carry, unused = lax.scan(advance, carry, (key_blocks, value_blocks))
    highest, totals, weighted = carry
    mixed = weighted / totals[:, :, None]
    return jnp.transpose(mixed, (1, 0, 2)).reshape(length, heads_here * HD).astype(jnp.bfloat16)


def expert_part(moe_tokens, expert_ids, gate_weights, up_weight, up_bias, down_weight, down_bias):
    tokens_here, width = moe_tokens.shape
    choose = expert_ids.shape[1]
    number = lax.axis_size("seq") * up_weight.shape[0]
    capacity = 5 * tokens_here // (2 * number)
    flat_ids = expert_ids.reshape(-1)
    hits = (flat_ids[:, None] == jnp.arange(number, dtype=jnp.int32)[None, :]).astype(jnp.int32)
    before = jnp.cumsum(hits, axis=0) - hits
    place = jnp.sum(before * hits, axis=1)
    slot = flat_ids * capacity + place
    slot_pairs = slot.reshape(tokens_here, choose)
    table = jnp.sum(
        (
            slot_pairs[None, :, :] == jnp.arange(number * capacity, dtype=jnp.int32)[:, None, None]
        ).astype(jnp.int32),
        axis=-1,
    )
    buffer = jnp.dot(
        table.astype(jnp.bfloat16), moe_tokens, preferred_element_type=jnp.float32
    ).astype(jnp.bfloat16)
    buffer = buffer.reshape(number, capacity, width)
    received = lax.all_to_all(buffer, "seq", split_axis=0, concat_axis=0, tiled=True)
    sources = received.shape[0]
    count = received.shape[1]
    flat_rows = received.reshape(sources * count, width)
    chip_rows = lax.all_gather(flat_rows, "tp", axis=0, tiled=True)

    def project(piece):
        return jax.nn.gelu(
            jnp.dot(chip_rows, piece[0], preferred_element_type=jnp.float32) + piece[1]
        ).astype(jnp.bfloat16)

    hidden = over_all_2(
        (up_weight[0], up_bias[0][None, :].astype(jnp.bfloat16)),
        "exp",
        1,
        lambda piece, start: project((piece[0], piece[1].astype(jnp.float32))),
    )
    down_whole = lax.all_gather(down_weight[0], "exp", axis=0, tiled=True)
    summed = lax.psum_scatter(
        jnp.dot(hidden, down_whole, preferred_element_type=jnp.float32).astype(jnp.bfloat16),
        "tp",
        scatter_dimension=0,
        tiled=True,
    ).astype(jnp.float32)
    result = (summed + down_bias[0][None, :]).astype(jnp.bfloat16).reshape(sources, count, width)
    returned = lax.all_to_all(result, "seq", split_axis=0, concat_axis=0, tiled=True)
    flat_out = returned.reshape(number * capacity, width)
    picked = flat_out[slot].reshape(tokens_here, choose, width).astype(jnp.float32)
    combined = jnp.sum(picked * gate_weights[:, :, None], axis=1)
    return combined.astype(jnp.bfloat16)


def local(
    attn_query,
    fresh_keys,
    fresh_values,
    stale_keys,
    stale_values,
    block_flags,
    moe_tokens,
    expert_ids,
    gate_weights,
    up_weight,
    up_bias,
    down_weight,
    down_bias,
):
    attn_out = attention_part(
        attn_query, fresh_keys, fresh_values, stale_keys, stale_values, block_flags
    )
    moe_out = expert_part(
        moe_tokens, expert_ids, gate_weights, up_weight, up_bias, down_weight, down_bias
    )
    return (attn_out, moe_out)


def solution(mesh):
    in_specs = (
        P(("groups", "seq"), ("exp", "tp")),
        P(("groups", "seq"), ("exp", "tp")),
        P(("groups", "seq"), ("exp", "tp")),
        P(("groups", "seq"), ("exp", "tp")),
        P(("groups", "seq"), ("exp", "tp")),
        P(("groups", "seq")),
        P(("groups", "seq", "exp", "tp"), None),
        P(("groups", "seq", "exp", "tp"), None),
        P(("groups", "seq", "exp", "tp"), None),
        P("seq", None, ("exp", "tp")),
        P("seq", ("exp", "tp")),
        P("seq", ("exp", "tp"), None),
        P("seq", None),
    )
    out_specs = (P(("groups", "seq"), ("exp", "tp")), P(("groups", "seq", "exp", "tp"), None))
    return jax.shard_map(local, mesh=mesh, in_specs=in_specs, out_specs=out_specs, check_vma=False)
```

profile of v0, /device:TPU:0, one launch (start us, length us, event | category | flops | bytes accessed | tf_op | source)
XLA Modules:
  0.0 262.1 jit_solution(10440550585438227936)
XLA Ops:
  7.2 0.0 copy-start
  7.2 0.0 all-gather.6.cloned.1.call-start
  7.2 0.8 copy.32
  8.0 0.1 eq.59
  8.2 0.1 eq.55
  8.3 1.2 reduce-window.6
  9.6 0.1 slice.10
  9.6 0.1 copy.35
  9.8 0.1 copy.36
  9.9 0.1 add_bitcast_fusion
  10.0 0.1 reduce_sum.41
  10.2 0.1 copy.37
  10.2 0.1 convert_reduce_fusion
  10.3 0.0 copy-done
  10.3 0.3 convolution_convert_fusion
  10.6 25.3 %all_to_all.10 = bf16[4,80,1152]{2,1,0:T(8,128)(2,1)} all-to-all(bf16[4,80,1152]{2,1,0:T(8,128)(2,1)S(1)} %bitcast.82), channel_id=1, replica_groups=mesh['groups'=2,'seq'=4,'exp'=2,'tp'=2] {'seq'}, dimensions={0} | all-to-all | bytes 1474560 | tf_op jit(solution)/shard_map/all_to_all | solution.py:84
  35.9 0.0 all-gather.6.cloned.1.call-update
  36.0 0.0 copy-start.5
  36.0 0.0 all-gather.8.cloned.1.call-start
  36.0 0.7 all-gather.8.cloned.1.call-update
  36.7 0.0 all-gather.10.cloned.1.call-start
  36.8 0.7 all-gather.10.cloned.1.call-update
  37.5 0.0 reduce-scatter.2.cloned.1.call-start
  37.5 0.0 copy-done.5
  37.5 4.4 %all_gather.22 = bf16[1,2304]{1,0:T(2,128)(2,1)S(1)} all-gather(bf16[1,1152]{1,0:T(2,128)(2,1)S(1)} %convert_element_type.61), channel_id=1, replica_groups=mesh['groups'=2,'seq'=4,'exp'=2,'tp'=2] {'exp'}, dimensions={1}, use_global_device_ids=true | all-gather | bytes 6912 | tf_op jit(solution)/shard_map/all_gather | solution.py:11
  41.9 3.0 %all-gather.6.cloned.1.call-done = bf16[640,1152]{1,0:T(8,128)(2,1)} async-done(((bf16[320,1152]{1,0:T(8,128)(2,1)}), bf16[640,1152]{1,0:T(8,128)(2,1)}) %all-gather.6.cloned.1.call-update) | async-done | bytes 1474576 | tf_op jit(solution)/shard_map/all_gather | solution.py:88
  44.9 72.0 %all-gather.8.cloned.1.call-done = bf16[1,1152,2304]{2,1,0:T(8,128)(2,1)} async-done(((bf16[1,1152,1152]{2,1,0:T(8,128)(2,1)}), bf16[1,1152,2304]{2,1,0:T(8,128)(2,1)}) %all-gather.8.cloned.1.call-update) | async-done | bytes 5308432 | tf_op jit(solution)/shard_map/all_gather | solution.py:11
  116.9 9.6 %fusion.22 = bf16[640,2304]{1,0:T(8,128)(2,1)} fusion(bf16[640,1152]{1,0:T(8,128)(2,1)} %all-gather.6.cloned.1.call-done, bf16[1,1152,2304]{2,1,0:T(8,128)(2,1)} %all-gather.8.cloned.1.call-done, f32[2304]{0:T(1024)S(1)} %convert_reduce_fusion.1), kind=kOutput, calls=%fused_computation.30 | convolution fusion | flops 3412131840 | bytes 9741312 | tf_op jit(solution)/shard_map/dot_general | solution.py:92
  126.5 0.0 copy-start.8
  126.5 0.0 copy-start.4
  126.5 61.3 %all-gather.10.cloned.1.call-done = bf16[1,2304,1152]{2,1,0:T(8,128)(2,1)} async-done(((bf16[1,1152,1152]{2,1,0:T(8,128)(2,1)}), bf16[1,2304,1152]{2,1,0:T(8,128)(2,1)}) %all-gather.10.cloned.1.call-update) | async-done | bytes 5308432 | tf_op jit(solution)/shard_map/all_gather | solution.py:101
  187.8 8.5 %fusion.29 = bf16[640,1152]{1,0:T(8,128)(2,1)} fusion(bf16[640,2304]{1,0:T(8,128)(2,1)} %fusion.22, bf16[1,2304,1152]{2,1,0:T(8,128)(2,1)} %all-gather.10.cloned.1.call-done), kind=kOutput, calls=%fused_computation.35 | convolution fusion | flops 3398123520 | bytes 9732096 | tf_op jit(solution)/shard_map/dot_general | solution.py:103
  196.3 0.0 reduce-scatter.2.cloned.1.call-update
  196.4 0.0 copy-done.8
  196.4 0.1 broadcast_bitcast_fusion
  196.5 0.0 copy-done.1
  196.5 0.0 copy-done.2
  196.5 0.0 copy-done.3
  196.5 0.0 copy-done.4
  196.5 16.5 %all_gather.18 = bf16[1024,288]{0,1:T(8,128)(2,1)S(1)} all-gather(bf16[256,288]{0,1:T(8,128)(2,1)S(1)} %get-tuple-element.101), channel_id=1, replica_groups=mesh['groups'=2,'seq'=4,'exp'=2,'tp'=2] {'seq'}, dimensions={0}, use_global_device_ids=true | all-gather | bytes 737280 | tf_op jit(solution)/shard_map/all_gather | solution.py:30
  213.1 0.4 reshape.94
  213.5 0.9 copy.30
  214.4 16.1 %all_gather.19 = bf16[1024,288]{0,1:T(8,128)(2,1)S(1)} all-gather(bf16[256,288]{0,1:T(8,128)(2,1)S(1)} %get-tuple-element.100), channel_id=1, replica_groups=mesh['groups'=2,'seq'=4,'exp'=2,'tp'=2] {'seq'}, dimensions={0}, use_global_device_ids=true | all-gather | bytes 737280 | tf_op jit(solution)/shard_map/all_gather | solution.py:31
  230.5 0.4 reshape.96
  230.9 0.9 copy.31
  231.8 0.0 copy-done.6
  231.8 0.0 reduce-scatter.2.cloned.1.call-done
  231.9 2.1 add_convert_fusion
  234.0 4.9 %all-to-all-start.1 = ((bf16[4,80,1152]{2,1,0:T(8,128)(2,1)}), bf16[4,80,1152]{2,1,0:T(8,128)(2,1)S(1)}, u32[]{:S(2)}, u32[]{:S(2)}) async-start(bf16[4,80,1152]{2,1,0:T(8,128)(2,1)} %bitcast.10), calls=%async_computation.2 | async-start | bytes 1474560 | tf_op jit(solution)/shard_map/all_to_all | solution.py:109
  238.8 6.9 %while.15 = (s32[]{:T(128)}, f32[4,256]{1,0:T(4,128)S(1)}, f32[4,256]{1,0:T(4,128)S(1)}, f32[4,256,72]{1,2,0:T(8,128)S(1)}, bf16[2,512,4,72]{1,3,2,0:T(8,128)(2,...) while((s32[]{:T(128)}, f32[4,256]{1,0:T(4,128)S(1)}, ...), condition=%wide.region_3.4_spmd.clone, body=%wide.region_0.3_spmd.clone.sunk | while | flops 155415552 | bytes 7685225 | solution.py:57
  238.8 1.5 bitcast_reduce_fusion.2
  240.4 0.4 fusion.49
  240.8 1.5 convolution_add_fusion.2
  242.3 1.5 bitcast_reduce_fusion.2
  243.8 0.4 fusion.49
  244.2 1.5 convolution_add_fusion.2
  245.7 0.1 mul.77
  245.8 0.0 copy-done.7
  245.8 0.1 copy.38
  246.0 0.7 divide_convert_fusion
  246.7 4.9 %all-to-all-done.1 = bf16[4,80,1152]{2,1,0:T(8,128)(2,1)S(1)} async-done(((bf16[4,80,1152]{2,1,0:T(8,128)(2,1)}), bf16[4,80,1152]{2,1,0:T(8,128)(2,1)S(1)}, u32[]{:S(2)}, u32[]{:S(2)}) %all-to-all-start.1) | async-done | bytes 737312 | tf_op jit(solution)/shard_map/all_to_all | solution.py:109
  251.6 1.3 gather_fusion
  252.8 0.6 reshape.103
  253.4 2.2 multiply_reduce_fusion
  (26 shorter events, 0.3 us)
Async XLA Ops:
  7.2 3.1 %copy-start = (bf16[128,1152]{1,0:T(8,128)(2,1)S(1)}, bf16[128,1152]{1,0:T(8,128)(2,1)}, u32[]{:S(2)}) copy-start(bf16[128,1152]{1,0:T(8,128)(2,1)} %param.21) | copy-start | bytes 884740
  7.2 37.7 %all-gather.6.cloned.1.call-start = ((), (), s32[]{:S(2)}) async-start(), calls=%async_computation.3 | async-start | bytes 2211840 | tf_op jit(solution)/shard_map/all_gather | solution.py:88
  36.0 1.5 copy-start.5
  36.0 80.9 %all-gather.8.cloned.1.call-start = ((), (), s32[]{:S(2)}) async-start(), calls=%async_computation.5 | async-start | bytes 7962624 | tf_op jit(solution)/shard_map/all_gather | solution.py:11
  36.7 151.0 %all-gather.10.cloned.1.call-start = ((), (), s32[]{:S(2)}) async-start(), calls=%async_computation.6 | async-start | bytes 7962624 | tf_op jit(solution)/shard_map/all_gather | solution.py:101
  37.5 194.4 %reduce-scatter.2.cloned.1.call-start = ((), (), s32[]{:S(2)}) async-start(), calls=%async_computation.4 | async-start | bytes 2211840 | tf_op jit(solution)/shard_map/reduce_scatter | solution.py:102
  126.5 69.9 %copy-start.8 = (s32[2]{0:T(128)S(1)}, s32[2]{0:T(128)}, u32[]{:S(2)}) copy-start(s32[2]{0:T(128)} %param.20) | copy-start | bytes 28
  126.5 70.0 %copy-start.1 = (bf16[256,288]{0,1:T(8,128)(2,1)S(1)}, bf16[256,288]{0,1:T(8,128)(2,1)}, u32[]{:S(2)}) copy-start(bf16[256,288]{0,1:T(8,128)(2,1)} %param.17) | copy-start | bytes 442372
  126.5 70.0 %copy-start.2 = (bf16[256,288]{0,1:T(8,128)(2,1)S(1)}, bf16[256,288]{0,1:T(8,128)(2,1)}, u32[]{:S(2)}) copy-start(bf16[256,288]{0,1:T(8,128)(2,1)} %param.19) | copy-start | bytes 442372
  126.5 70.0 %copy-start.3 = (bf16[256,288]{0,1:T(8,128)(2,1)S(1)}, bf16[256,288]{0,1:T(8,128)(2,1)}, u32[]{:S(2)}) copy-start(bf16[256,288]{0,1:T(8,128)(2,1)} %param.16) | copy-start | bytes 442372
  126.5 70.0 %copy-start.4 = (bf16[256,288]{0,1:T(8,128)(2,1)S(1)}, bf16[256,288]{0,1:T(8,128)(2,1)}, u32[]{:S(2)}) copy-start(bf16[256,288]{0,1:T(8,128)(2,1)} %param.18) | copy-start | bytes 442372
  213.1 18.7 %copy-start.6 = (f32[1,1152]{1,0:T(1,128)S(1)}, f32[1,1152]{1,0:T(1,128)}, u32[]{:S(2)}) copy-start(f32[1,1152]{1,0:T(1,128)} %param.27) | copy-start | bytes 13828
  234.0 17.6 %all-to-all-start.1 = ((bf16[4,80,1152]{2,1,0:T(8,128)(2,1)}), bf16[4,80,1152]{2,1,0:T(8,128)(2,1)S(1)}, u32[]{:S(2)}, u32[]{:S(2)}) async-start(bf16[4,80,1152]{2,1,0:T(8,128)(2,1)} %bitcast.10), calls=%async_computation.2 | async-start | bytes 1474560 | tf_op jit(solution)/shard_map/all_to_all | solution.py:109
  238.8 7.0 %copy-start.7 = (f32[128,2]{0,1:T(2,128)S(1)}, f32[128,2]{0,1:T(2,128)}, u32[]{:S(2)}) copy-start(f32[128,2]{0,1:T(2,128)} %param.23) | copy-start | bytes 3076
Sparse Core Ops, SparseCore 0:
  36.1 8.7 all-gather.5
  46.4 70.4 all-gather.7
  118.5 69.2 all-gather.9
  196.5 8.9 reduce-scatter.1
where the time goes:
time: 263 us; the launch traced here: 262 us
  waiting for transfers between devices  143 us (54%)
  blocking collectives  62.3 us (24%)
  matrix products  24.4 us (9%)
  between operations  14 us (5%)
  other arithmetic  7.3 us (3%)
  local copies, waits for them, and re-layouts  6.41 us (2%)
  starting transfers between devices  5.02 us (2%)
    all_gather x1, waiting for transfers between devices, over_all_2(): everything = lax.all_gather(share, axis, axis=dim, tiled=True)  72 us
    all_gather x1, waiting for transfers between devices, expert_part(): down_whole = lax.all_gather(down_weight[0], 'exp', axis=0, tiled=True)  61.3 us
    all_to_all x1, blocking collectives, expert_part(): lax.all_to_all(buffer, 'seq', split_axis=0, concat_axis=0, tiled=True)  25.3 us
    all_gather x1, blocking collectives, attention_part(): lax.all_gather(keys, 'seq', axis=0, tiled=True)  16.5 us
    all_gather x1, blocking collectives, attention_part(): lax.all_gather(values, 'seq', axis=0, tiled=True)  16.1 us
    dot_general x1, matrix products, project(): jnp.dot(chip_rows, piece[0], preferred_element_type=jnp.float32) + piece[1]  9.57 us
    dot_general x1, matrix products, expert_part(): jnp.dot(hidden, down_whole, preferred_element_type=jnp.float32)  8.54 us
  transfers between devices with their start and end apart: 5, of which 4 were waited for; matrix products, arithmetic and copies ran while one was open for 8% of the time, Pallas kernels for 0%

commit v1 on v0

--- a/solution.py
+++ b/solution.py
@@ -5,6 +5,24 @@
 from jax.sharding import PartitionSpec as P
 
 HD = 72
+
+
+def ring_gather(array, axis, dim):
+    ways, here, step = (lax.axis_size(axis), lax.axis_index(axis), array.shape[dim])
+    lengths = [n * ways if d == dim else n for d, n in enumerate(array.shape)]
+    full = lax.dynamic_update_slice_in_dim(
+        jnp.zeros(lengths, array.dtype), array, here * step, axis=dim
+    )
+    going_up = going_down = array
+    for far in range(1, ways // 2 + 1):
+        going_up = lax.ppermute(going_up, axis, [(d, (d + 1) % ways) for d in range(ways)])
+        full = lax.dynamic_update_slice_in_dim(full, going_up, (here - far) % ways * step, axis=dim)
+        if 2 * far < ways:
+            going_down = lax.ppermute(going_down, axis, [(d, (d - 1) % ways) for d in range(ways)])
+            full = lax.dynamic_update_slice_in_dim(
+                full, going_down, (here + far) % ways * step, axis=dim
+            )
+    return full
 
 
 def over_all_2(share, axis, dim, apply):
@@ -26,10 +44,7 @@
         jnp.zeros((heads_here, length, HD), jnp.float32),
     )
     carry = initial
-    piece = (
-        lax.all_gather(keys, "seq", axis=0, tiled=True),
-        lax.all_gather(values, "seq", axis=0, tiled=True),
-    )
+    piece = (ring_gather(keys, "seq", 0), lax.all_gather(values, "seq", axis=0, tiled=True))
     count = piece[0].shape[0]
     width = math.gcd(count, 512)
     key_blocks = piece[0].reshape(count // width, width, heads_here, HD)

time: 263 us -> 260 us (0.989)
  blocking collectives: 62.3 us -> 47.7 us
  waiting for transfers between devices: 143 us -> 151 us
  starting transfers between devices: 5.02 us -> 8.43 us
    all_gather x1 -> x0, blocking collectives: 16.5 us -> none  [attention_part(): lax.all_gather(keys, 'seq', axis=0, tiled=True)]
    ppermute x0 -> x3, waiting for transfers between devices: none -> 6.22 us  [the longest x2 6.22 us: ring_gather(): lax.ppermute(going_up, axis, [(d, (d + 1) % ways) for d in range(ways)])]
    ppermute x0 -> x3, starting transfers between devices: none -> 4.6 us  [the longest x1 2.34 us: ring_gather(): lax.ppermute(going_down, axis, [(d, (d - 1) % ways) for d in range(ways)])]
  transfers between devices with their start and end apart: 5 -> 8, of which waited for: 4 -> 5; matrix products, arithmetic and copies ran while one was open for 8% -> 8% of each run, Pallas kernels for 0% -> 0%
where the time goes in v1:
time: 260 us
  waiting for transfers between devices  151 us (58%)
  blocking collectives  47.7 us (18%)
  matrix products  24.4 us (9%)
  between operations  14.1 us (5%)
  starting transfers between devices  8.43 us (3%)
  other arithmetic  7.36 us (3%)
  local copies, waits for them, and re-layouts  6.53 us (3%)
    all_gather x1, waiting for transfers between devices, over_all_2(): everything = lax.all_gather(share, axis, axis=dim, tiled=True)  72 us
    all_gather x1, waiting for transfers between devices, expert_part(): down_whole = lax.all_gather(down_weight[0], 'exp', axis=0, tiled=True)  61.2 us
    all_to_all x1, blocking collectives, expert_part(): lax.all_to_all(buffer, 'seq', split_axis=0, concat_axis=0, tiled=True)  25.3 us
    all_gather x1, blocking collectives, attention_part(): lax.all_gather(values, 'seq', axis=0, tiled=True)  18 us
    dot_general x1, matrix products, project(): jnp.dot(chip_rows, piece[0], preferred_element_type=jnp.float32) + piece[1]  9.58 us
    dot_general x1, matrix products, expert_part(): jnp.dot(hidden, down_whole, preferred_element_type=jnp.float32)  8.54 us
    all_to_all x1, waiting for transfers between devices, expert_part(): lax.all_to_all(result, 'seq', split_axis=0, concat_axis=0, tiled=True)  7.02 us
    ppermute x2, waiting for transfers between devices, ring_gather(): lax.ppermute(going_up, axis, [(d, (d + 1) % ways) for d in range(ways)])  6.22 us
  transfers between devices with their start and end apart: 8, of which 5 were waited for; matrix products, arithmetic and copies ran while one was open for 8% of the time, Pallas kernels for 0%

profile of v1, /device:TPU:0, one launch (start us, length us, event | category | flops | bytes accessed | tf_op | source)
XLA Modules:
  0.0 259.5 jit_solution(17759264908889127979)
XLA Ops:
  7.2 0.0 copy-start
  7.2 0.0 all-gather.6.cloned.1.call-start
  7.2 0.8 copy.32
  8.0 0.1 eq.63
  8.2 0.1 eq.59
  8.3 1.2 reduce-window.6
  9.6 0.1 slice.10
  9.6 0.1 copy.35
  9.8 0.1 copy.36
  9.9 0.1 add_bitcast_fusion
  10.0 0.1 reduce_sum.41
  10.2 0.1 copy.37
  10.2 0.1 convert_reduce_fusion
  10.3 0.3 convolution_convert_fusion
  10.6 25.3 %all_to_all.10 = bf16[4,80,1152]{2,1,0:T(8,128)(2,1)} all-to-all(bf16[4,80,1152]{2,1,0:T(8,128)(2,1)S(1)} %bitcast.82), channel_id=1, replica_groups=mesh['groups'=2,'seq'=4,'exp'=2,'tp'=2] {'seq'}, dimensions={0} | all-to-all | bytes 1474560 | tf_op jit(solution)/shard_map/all_to_all | solution.py:99
  35.9 0.0 all-gather.6.cloned.1.call-update
  36.0 0.0 copy-start.5
  36.0 0.0 all-gather.8.cloned.1.call-start
  36.0 0.7 all-gather.8.cloned.1.call-update
  36.7 0.0 all-gather.10.cloned.1.call-start
  36.8 0.7 all-gather.10.cloned.1.call-update
  37.5 0.0 reduce-scatter.2.cloned.1.call-start
  37.5 4.4 %all_gather.18 = bf16[1,2304]{1,0:T(2,128)(2,1)S(1)} all-gather(bf16[1,1152]{1,0:T(2,128)(2,1)S(1)} %convert_element_type.61), channel_id=1, replica_groups=mesh['groups'=2,'seq'=4,'exp'=2,'tp'=2] {'exp'}, dimensions={1}, use_global_device_ids=true | all-gather | bytes 6912 | tf_op jit(solution)/shard_map/all_gather | solution.py:29
  41.9 3.0 %all-gather.6.cloned.1.call-done = bf16[640,1152]{1,0:T(8,128)(2,1)} async-done(((bf16[320,1152]{1,0:T(8,128)(2,1)}), bf16[640,1152]{1,0:T(8,128)(2,1)}) %all-gather.6.cloned.1.call-update) | async-done | bytes 1474576 | tf_op jit(solution)/shard_map/all_gather | solution.py:103
  44.9 72.0 %all-gather.8.cloned.1.call-done = bf16[1,1152,2304]{2,1,0:T(8,128)(2,1)} async-done(((bf16[1,1152,1152]{2,1,0:T(8,128)(2,1)}), bf16[1,1152,2304]{2,1,0:T(8,128)(2,1)}) %all-gather.8.cloned.1.call-update) | async-done | bytes 5308432 | tf_op jit(solution)/shard_map/all_gather | solution.py:29
  116.9 9.6 %fusion.22 = bf16[640,2304]{1,0:T(8,128)(2,1)} fusion(bf16[640,1152]{1,0:T(8,128)(2,1)} %all-gather.6.cloned.1.call-done, bf16[1,1152,2304]{2,1,0:T(8,128)(2,1)} %all-gather.8.cloned.1.call-done, f32[2304]{0:T(1024)S(1)} %convert_reduce_fusion.1), kind=kOutput, calls=%fused_computation.30 | convolution fusion | flops 3412131840 | bytes 9741312 | tf_op jit(solution)/shard_map/dot_general | solution.py:107
  126.5 0.0 copy-start.4
  126.5 61.2 %all-gather.10.cloned.1.call-done = bf16[1,2304,1152]{2,1,0:T(8,128)(2,1)} async-done(((bf16[1,1152,1152]{2,1,0:T(8,128)(2,1)}), bf16[1,2304,1152]{2,1,0:T(8,128)(2,1)}) %all-gather.10.cloned.1.call-update) | async-done | bytes 5308432 | tf_op jit(solution)/shard_map/all_gather | solution.py:116
  187.8 8.5 %fusion.29 = bf16[640,1152]{1,0:T(8,128)(2,1)} fusion(bf16[640,2304]{1,0:T(8,128)(2,1)} %fusion.22, bf16[1,2304,1152]{2,1,0:T(8,128)(2,1)} %all-gather.10.cloned.1.call-done), kind=kOutput, calls=%fused_computation.35 | convolution fusion | flops 3398123520 | bytes 9732096 | tf_op jit(solution)/shard_map/dot_general | solution.py:118
  196.3 0.0 reduce-scatter.2.cloned.1.call-update
  196.3 0.0 copy-start.7
  196.4 0.0 copy-start.6
  196.4 0.0 copy-done.8
  196.4 0.1 broadcast_bitcast_fusion
  196.5 0.1 broadcast_in_dim.37
  196.5 0.0 copy-done.1
  196.6 0.1 constant_dynamic-update-slice_fusion.3
  196.7 1.5 collective-permute-start
  198.2 2.3 collective-permute-start.1
  200.5 0.1 mul.93
  200.7 18.0 %all_gather.15 = bf16[1024,288]{0,1:T(8,128)(2,1)S(1)} all-gather(bf16[256,288]{0,1:T(8,128)(2,1)S(1)} %get-tuple-element.102), channel_id=1, replica_groups=mesh['groups'=2,'seq'=4,'exp'=2,'tp'=2] {'seq'}, dimensions={0}, use_global_device_ids=true | all-gather | bytes 737280 | tf_op jit(solution)/shard_map/all_gather | solution.py:47
  218.7 0.4 reshape.96
  219.2 0.9 copy.31
  220.0 0.1 copy.38
  220.2 0.0 collective-permute-done
  220.2 0.7 collective-permute-start.2
  221.0 0.0 collective-permute-done.1
  221.0 6.2 %collective-permute-done.2 = bf16[256,288]{0,1:T(8,128)(2,1)S(1)} collective-permute-done((bf16[256,288]{0,1:T(8,128)(2,1)S(1)}, bf16[256,288]{0,1:T(8,128)(2,1)S(1)}, u32[]{:S(2)}, u32[]{:S(2)}) %collective-permute-start.2) | collective-permute-done | bytes 147488 | tf_op jit(solution)/shard_map/ppermute | solution.py:18
  227.2 0.4 reshape.94
  227.7 0.9 copy.30
  228.6 2.1 add_convert_fusion
  230.7 3.7 %all-to-all-start.1 = ((bf16[4,80,1152]{2,1,0:T(8,128)(2,1)}), bf16[4,80,1152]{2,1,0:T(8,128)(2,1)S(1)}, u32[]{:S(2)}, u32[]{:S(2)}) async-start(bf16[4,80,1152]{2,1,0:T(8,128)(2,1)} %bitcast.10), calls=%async_computation.2 | async-start | bytes 1474560 | tf_op jit(solution)/shard_map/all_to_all | solution.py:124
  234.4 6.9 %while.15 = (s32[]{:T(128)}, f32[4,256]{1,0:T(4,128)S(1)}, f32[4,256]{1,0:T(4,128)S(1)}, f32[4,256,72]{1,2,0:T(8,128)S(1)}, bf16[2,512,4,72]{1,3,2,0:T(8,128)(2,...) while((s32[]{:T(128)}, f32[4,256]{1,0:T(4,128)S(1)}, ...), condition=%wide.region_3.4_spmd.clone, body=%wide.region_0.3_spmd.clone.sunk | while | flops 155415552 | bytes 7685225 | solution.py:72
  234.4 1.5 bitcast_reduce_fusion.2
  235.9 0.4 fusion.49
  236.3 1.5 convolution_add_fusion.2
  237.8 1.5 bitcast_reduce_fusion.2
  239.3 0.4 fusion.49
  239.7 1.5 convolution_add_fusion.2
  241.2 0.7 divide_convert_fusion
  241.9 7.0 %all-to-all-done.1 = bf16[4,80,1152]{2,1,0:T(8,128)(2,1)S(1)} async-done(((bf16[4,80,1152]{2,1,0:T(8,128)(2,1)}), bf16[4,80,1152]{2,1,0:T(8,128)(2,1)S(1)}, u32[]{:S(2)}, u32[]{:S(2)}) %all-to-all-start.1) | async-done | bytes 737312 | tf_op jit(solution)/shard_map/all_to_all | solution.py:124
  248.9 1.3 gather_fusion
  250.2 0.6 reshape.103
  250.8 2.2 multiply_reduce_fusion
  (35 shorter events, 0.3 us)
Async XLA Ops:
  7.2 3.1 %copy-start = (bf16[128,1152]{1,0:T(8,128)(2,1)S(1)}, bf16[128,1152]{1,0:T(8,128)(2,1)}, u32[]{:S(2)}) copy-start(bf16[128,1152]{1,0:T(8,128)(2,1)} %param.21) | copy-start | bytes 884740
  7.2 37.7 %all-gather.6.cloned.1.call-start = ((), (), s32[]{:S(2)}) async-start(), calls=%async_computation.3 | async-start | bytes 2211840 | tf_op jit(solution)/shard_map/all_gather | solution.py:103
  36.0 1.5 copy-start.5
  36.0 80.9 %all-gather.8.cloned.1.call-start = ((), (), s32[]{:S(2)}) async-start(), calls=%async_computation.5 | async-start | bytes 7962624 | tf_op jit(solution)/shard_map/all_gather | solution.py:29
  36.7 151.0 %all-gather.10.cloned.1.call-start = ((), (), s32[]{:S(2)}) async-start(), calls=%async_computation.6 | async-start | bytes 7962624 | tf_op jit(solution)/shard_map/all_gather | solution.py:116
  37.5 191.1 %reduce-scatter.2.cloned.1.call-start = ((), (), s32[]{:S(2)}) async-start(), calls=%async_computation.4 | async-start | bytes 2211840 | tf_op jit(solution)/shard_map/reduce_scatter | solution.py:117
  126.5 69.9 %copy-start.8 = (s32[2]{0:T(128)S(1)}, s32[2]{0:T(128)}, u32[]{:S(2)}) copy-start(s32[2]{0:T(128)} %param.20) | copy-start | bytes 28
  126.5 70.0 %copy-start.1 = (bf16[256,288]{0,1:T(8,128)(2,1)S(1)}, bf16[256,288]{0,1:T(8,128)(2,1)}, u32[]{:S(2)}) copy-start(bf16[256,288]{0,1:T(8,128)(2,1)} %param.16) | copy-start | bytes 442372
  126.5 70.0 %copy-start.2 = (bf16[256,288]{0,1:T(8,128)(2,1)S(1)}, bf16[256,288]{0,1:T(8,128)(2,1)}, u32[]{:S(2)}) copy-start(bf16[256,288]{0,1:T(8,128)(2,1)} %param.18) | copy-start | bytes 442372
  126.5 70.1 %copy-start.3 = (bf16[256,288]{0,1:T(8,128)(2,1)S(1)}, bf16[256,288]{0,1:T(8,128)(2,1)}, u32[]{:S(2)}) copy-start(bf16[256,288]{0,1:T(8,128)(2,1)} %param.17) | copy-start | bytes 442372
  126.5 70.1 %copy-start.4 = (bf16[256,288]{0,1:T(8,128)(2,1)S(1)}, bf16[256,288]{0,1:T(8,128)(2,1)}, u32[]{:S(2)}) copy-start(bf16[256,288]{0,1:T(8,128)(2,1)} %param.19) | copy-start | bytes 442372
  196.3 23.7 %copy-start.7 = (f32[128,2]{0,1:T(2,128)S(1)}, f32[128,2]{0,1:T(2,128)}, u32[]{:S(2)}) copy-start(f32[128,2]{0,1:T(2,128)} %param.23) | copy-start | bytes 3076
  196.4 23.8 %copy-start.6 = (f32[1,1152]{1,0:T(1,128)S(1)}, f32[1,1152]{1,0:T(1,128)}, u32[]{:S(2)}) copy-start(f32[1,1152]{1,0:T(1,128)} %param.27) | copy-start | bytes 13828
  196.7 23.5 %collective-permute-start = (bf16[256,288]{0,1:T(8,128)(2,1)S(1)}, bf16[256,288]{0,1:T(8,128)(2,1)S(1)}, u32[]{:S(2)}, u32[]{:S(2)}) collective-permute-start(bf16[256,288]{0,1:T(8,128)(2,1)S(1)} %get-tuple-element.97), channel_id=1, source_target_pairs={{0,4},{4,8},{8,12},{12,0},{1,5},{5,9},{9,13},{13,1},{2,6},{6,10},{... | collective-permute-start | bytes 442376 | tf_op jit(solution)/shard_map/ppermute | solution.py:18
  198.2 22.8 %collective-permute-start.1 = (bf16[256,288]{0,1:T(8,128)(2,1)S(1)}, bf16[256,288]{0,1:T(8,128)(2,1)S(1)}, u32[]{:S(2)}, u32[]{:S(2)}) collective-permute-start(bf16[256,288]{0,1:T(8,128)(2,1)S(1)} %get-tuple-element.97), channel_id=1, source_target_pairs={{0,12},{4,0},{8,4},{12,8},{1,13},{5,1},{9,5},{13,9},{2,14},{6,2},{... | collective-permute-start | bytes 442376 | tf_op jit(solution)/shard_map/ppermute | solution.py:21
  220.2 7.0 %collective-permute-start.2 = (bf16[256,288]{0,1:T(8,128)(2,1)S(1)}, bf16[256,288]{0,1:T(8,128)(2,1)S(1)}, u32[]{:S(2)}, u32[]{:S(2)}) collective-permute-start(bf16[256,288]{0,1:T(8,128)(2,1)S(1)} %collective-permute-done), channel_id=1, source_target_pairs={{0,4},{4,8},{8,12},{12,0},{1,5},{5,9},{9,13},{13,1},{2,6},{6,10},{... | collective-permute-start | bytes 442376 | tf_op jit(solution)/shard_map/ppermute | solution.py:18
  230.7 18.2 %all-to-all-start.1 = ((bf16[4,80,1152]{2,1,0:T(8,128)(2,1)}), bf16[4,80,1152]{2,1,0:T(8,128)(2,1)S(1)}, u32[]{:S(2)}, u32[]{:S(2)}) async-start(bf16[4,80,1152]{2,1,0:T(8,128)(2,1)} %bitcast.10), calls=%async_computation.2 | async-start | bytes 1474560 | tf_op jit(solution)/shard_map/all_to_all | solution.py:124
Sparse Core Ops, SparseCore 0:
  36.1 8.7 all-gather.5
  46.4 70.4 all-gather.7
  118.5 69.2 all-gather.9
  196.5 8.8 reduce-scatter.1
